TPU v7x, 32 devices: a whole 2x2x4 slice. The times are simulated.
32 devices in a mesh: lat: 8 (over y, x, core), lev: 4 (over z).
Axes of the slice: x: 2, y: 2, z: 4, core: 2. Of those that a mesh axis runs over, the one named last changes fastest.
Arguments:
- fields: float32 [12, 128, 256, 1024], P(None, 'lev', 'lat'), may hold values from -6 to 6
- legendre: bfloat16 [256, 256, 256], P('lat'), as said below
- owner_counts: int32 [8], replicated, may hold values from 1 to 64, 256 in all
Outputs:
- covariance: float32 [512, 128, 128], P('lat', 'lev')
Inputs may be any that keep to these rules, and one draw needn't show every extreme that they name: `owner_counts`: each owner holds 1 to 64 total wavenumbers, the counts sum to 256, and some owner holds exactly 64. legendre[lat, m, n] is zero where n < m.
All inputs are finite; a program needn't handle non-finite values.
Results may differ from a plain program's by a relative error of at most 0.0038.
Values may be sent and summed in bfloat16 or wider, within the bound.
A program may use at most 192 MiB of HBM per device.

v0:
```python
import math

import jax
import jax.numpy as jnp
from jax import lax
from jax.sharding import PartitionSpec as P


def fourier_table(points, modes):
    places = jnp.arange(points, dtype=jnp.int32)
    orders = jnp.arange(modes, dtype=jnp.int32)
    phase = places[:, None] * orders[None, :] % points
    angle = phase.astype(jnp.float32) * (2.0 * math.pi / points)
    factor = points ** (-0.5)
    return jnp.stack([jnp.cos(angle) * factor, -jnp.sin(angle) * factor], axis=2)


def on_device(fields, legendre, owner_counts):
    members, lev_rows, lat_rows, points = fields.shape
    modes = legendre.shape[1]
    lev_count = lax.axis_size("lev")
    owners = owner_counts.shape[0]
    capacity = 2 * modes // owners
    dft_table = fourier_table(points, modes)
    spectra = jnp.einsum("belx,xmc->lmcbe", fields, dft_table, precision=lax.Precision.HIGHEST)
    spectra = spectra.reshape(lat_rows, modes, 2 * members * lev_rows).astype(jnp.bfloat16)
    collected_rows, transform_table_rows = (
        lax.all_to_all(spectra, "lat", split_axis=1, concat_axis=0, tiled=True),
        lax.all_to_all(legendre, "lat", split_axis=1, concat_axis=0, tiled=True),
    )
    wavenumber_rows = jnp.einsum(
        "dez,det->tez", collected_rows, transform_table_rows, preferred_element_type=jnp.float32
    )
    resident_modes = wavenumber_rows.shape[1]
    shaped = wavenumber_rows.reshape(modes, resident_modes, 2, members, lev_rows)
    anomaly = (shaped - jnp.mean(shaped, axis=3, keepdims=True)).astype(jnp.bfloat16)
    anomaly = anomaly.reshape(modes, resident_modes, 2 * members * lev_rows)
    starts = jnp.cumsum(owner_counts) - owner_counts
    offset = jnp.arange(capacity, dtype=jnp.int32)
    active_flag = offset[None, :] < owner_counts[:, None]
    slot_index = jnp.where(active_flag, starts[:, None] + offset[None, :], 0).reshape(-1)
    slotted = jnp.take(anomaly, slot_index, axis=0)
    slotted = jnp.where(active_flag.reshape(-1)[:, None, None], slotted, jnp.zeros_like(slotted))
    slotted = slotted[None]
    received = lax.all_to_all(
        lax.all_to_all(slotted, "lat", split_axis=1, concat_axis=2, tiled=True),
        "lev",
        split_axis=2,
        concat_axis=0,
        tiled=True,
    )
    mode_share = received.shape[2]
    blocks = received.reshape(lev_count, capacity, mode_share, 2 * members, lev_rows)
    partial_value = jnp.einsum(
        "esaql,fsaqk->selfk", blocks, blocks, preferred_element_type=jnp.float32
    )
    partial_value = partial_value.reshape(capacity, lev_count * lev_rows, lev_count * lev_rows)
    summed = lax.psum_scatter(partial_value, "lev", scatter_dimension=1, tiled=True)
    owner = lax.axis_index("lat")
    wavenumber = starts[owner] + offset
    live_count = owner_counts[owner]
    divisor = ((members - 1) * (2 * wavenumber + 2)).astype(jnp.float32)
    scaled = summed / divisor[:, None, None]
    return jnp.where((offset < live_count)[:, None, None], scaled, jnp.zeros_like(scaled))


def solution(mesh):
    return jax.shard_map(
        on_device,
        mesh=mesh,
        in_specs=(P(None, "lev", "lat", None), P("lat", None, None), P()),
        out_specs=P("lat", "lev", None),
        check_vma=False,
    )
```

profile of v0, /device:TPU:0, one launch (start us, length us, event | category | flops | bytes accessed | tf_op | source)
XLA Modules:
  0.0 1535.6 jit_solution(14930532763259418552)
XLA Ops:
  6.5 6.5 copy.18
  13.0 5.2 all-to-all-start.1
  18.2 4.2 negate_multiply_fusion
  22.4 84.9 %fusion.7 = bf16[256,2,12,32,32]{0,4,3,2,1:T(8,128)(2,1)} fusion(f32[12,32,32,1024]{3,2,1,0:T(8,128)} %param.3, f32[1024,256,1]{1,0,2:T(8,128)S(1)} %get-tuple-element.7, f32[1024,256,1]{1,0,2:T(8,128)S(1)} %get-tuple-element.8), kind=kOutput, calls=%fused_computation.11 | convolution fusion | flops 77316227072 | bytes 65011712 | tf_op jit(solution)/shard_map/belx,xmc->lmcbe/dot_general | solution.py:25
  107.3 18.2 %copy.15 = bf16[32,256,768]{2,0,1:T(8,128)(2,1)} copy(bf16[32,256,768]{1,0,2:T(8,128)(2,1)} %bitcast.76) | data formatting | bytes 25165824 | tf_op jit(solution)/shard_map/convert_element_type | solution.py:26
  125.6 0.0 copy-start
  125.6 0.0 all-to-all-done.1
  125.6 5.5 all-to-all-start
  131.1 0.3 reduce-scatter.2.cloned.1.call-start
  131.3 0.0 copy-done
  131.4 0.2 reduce-window.9
  131.6 0.0 copy-start.2
  131.6 0.1 iota_add_fusion
  131.6 0.4 copy-done.2
  132.1 0.1 select_n.90
  132.1 0.1 add.91
  132.2 0.1 iota_compare_fusion
  132.3 0.1 lt.78
  132.4 4.8 copy.19
  137.2 132.9 %all-to-all-done = bf16[32,256,768]{2,0,1:T(8,128)(2,1)} async-done(((bf16[32,256,768]{2,0,1:T(8,128)(2,1)}), bf16[32,256,768]{2,0,1:T(8,128)(2,1)}, u32[]{:S(2)}, u32[]{:S(2)}) %all-to-all-start) | async-done | bytes 12582944 | tf_op jit(solution)/shard_map/all_to_all | solution.py:28
  270.1 14.1 copy.17
  284.1 20.2 %fusion.5 = f32[32,768,256]{2,1,0:T(8,128)} fusion(bf16[256,32,256]{2,0,1:T(8,128)(2,1)} %bitcast.75, bf16[256,32,768]{2,1,0:T(8,128)(2,1)} %bitcast.71), kind=kOutput, calls=%fused_computation.8 | convolution fusion | flops 3221225472 | bytes 41943040 | tf_op jit(solution)/shard_map/dez,det->tez/dot_general | solution.py:31
  304.4 10.0 reduce_sum.9
  314.4 0.2 broadcast_multiply_fusion
  314.6 15.0 fusion.4
  329.6 16.8 %copy.21 = bf16[256,32,768]{2,1,0:T(8,128)(2,1)} copy(bf16[256,32,768]{0,2,1:T(8,128)(2,1)} %fusion.4) | data formatting | bytes 25165824 | tf_op jit(solution)/shard_map/convert_element_type | solution.py:36
  346.4 20.7 %gather_fusion = bf16[512,32,768]{2,1,0:T(8,128)(2,1)} fusion(bf16[256,32,768]{2,1,0:T(8,128)(2,1)} %copy.21, s32[1024]{0:T(1024)S(1)} %pad_clamp_fusion), kind=kCustom, calls=%fused_computation | custom fusion | bytes 50333696 | tf_op jit(solution)/shard_map/jit(_take)/gather | solution.py:42
  367.1 22.1 %fusion.3 = bf16[1,512,32,768]{3,2,0,1:T(8,128)(2,1)} fusion(bf16[512,32,768]{2,1,0:T(8,128)(2,1)} %gather_fusion, pred[512]{0:T(512)(128)(4,1)S(1)} %compare_and_fusion, pred[512]{0:T(512)(128)(4,1)S(1)} %lt.78), kind=kLoop, calls=%fused_computation.5 | loop fusion | flops 25165824 | bytes 50332672 | tf_op jit(solution)/shard_map/jit(_where)/select_n | solution.py:43
  389.2 278.2 %all_to_all.69 = bf16[1,512,32,768]{3,2,0,1:T(8,128)(2,1)S(1)} all-to-all(bf16[1,512,32,768]{3,2,0,1:T(8,128)(2,1)} %fusion.3), channel_id=1, replica_groups=mesh['lat'=8,'lev'=4] {'lat'}, dimensions={1} | all-to-all | bytes 50331648 | tf_op jit(solution)/shard_map/all_to_all | solution.py:46
  667.4 8.7 copy.23
  676.0 23.2 %copy.24 = bf16[1,64,256,768]{3,1,0,2:T(8,128)(2,1)S(1)} copy(bf16[1,64,256,768]{3,2,1,0:T(8,128)(2,1)} %bitcast.69) | data formatting | bytes 50331648 | tf_op jit(solution)/shard_map/all_to_all | solution.py:46
  699.3 548.4 %all_to_all.70 = bf16[1,64,256,768]{3,1,0,2:T(8,128)(2,1)} all-to-all(bf16[1,64,256,768]{3,1,0,2:T(8,128)(2,1)S(1)} %copy.24), channel_id=1, replica_groups=mesh['lat'=8,'lev'=4] {'lev'}, dimensions={2} | all-to-all | bytes 50331648 | tf_op jit(solution)/shard_map/all_to_all | solution.py:45
  1247.7 23.9 %copy.25 = bf16[1,64,256,768]{3,2,1,0:T(8,128)(2,1)} copy(bf16[1,64,256,768]{3,1,0,2:T(8,128)(2,1)} %all_to_all.70) | data formatting | bytes 50331648 | tf_op jit(solution)/shard_map/all_to_all | solution.py:45
  1271.6 44.6 %copy.26 = bf16[4,1,64,64,768]{3,4,0,2,1:T(8,128)(2,1)} copy(bf16[4,1,64,64,768]{4,3,0,2,1:T(8,128)(2,1)} %bitcast.70) | data formatting | bytes 50331648 | tf_op jit(solution)/shard_map/all_to_all | solution.py:45
  1316.2 50.3 %convolution_bitcast_fusion = f32[64,4,32,4,32]{4,2,3,1,0:T(8,128)} fusion(bf16[4,64,64,24,32,1]{2,4,3,5,0,1:T(8,128)(2,1)} %bitcast.72, bf16[4,64,64,24,32,1]{2,4,3,0,5,1:T(8,128)(2,1)} %bitcast.73), kind=kOutput, calls=%fused_computation.10 | convolution fusion | flops 3221225472 | bytes 54525952 | tf_op jit(solution)/shard_map/esaql,fsaqk->selfk/dot_general | solution.py:54
  1366.5 0.0 copy-start.3
  1366.5 0.0 copy-start.1
  1366.5 14.6 copy.27
  1381.2 0.0 reduce-scatter.2.cloned.1.call-update
  1381.2 0.0 copy-done.3
  1381.2 0.6 dynamic_slice.7
  1381.8 0.0 copy-done.1
  1381.8 0.6 dynamic_slice.6
  1382.4 0.7 multiply_convert_fusion
  1383.0 0.6 iota_compare_fusion.1
  1383.6 141.1 %reduce-scatter.2.cloned.1.call-done = f32[64,32,128]{0,2,1:T(8,128)} async-done(((f32[64,128,128]{0,2,1:T(8,128)}), f32[64,32,128]{0,2,1:T(8,128)}) %reduce-scatter.2.cloned.1.call-update) | async-done | bytes 1048592 | tf_op jit(solution)/shard_map/reduce_scatter | solution.py:58
  1524.7 1.8 divide_select_fusion
  1526.5 1.8 copy.28
  (4 shorter events, 0.0 us)
Async XLA Ops:
  13.0 112.5 %all-to-all-start.1 = ((bf16[32,256,256]{2,0,1:T(8,128)(2,1)}), bf16[32,256,256]{2,0,1:T(8,128)(2,1)}, u32[]{:S(2)}, u32[]{:S(2)}) async-start(bf16[32,256,256]{2,0,1:T(8,128)(2,1)} %copy.18), calls=%async_computation.1 | async-start | bytes 8388608 | tf_op jit(solution)/shard_map/all_to_all | solution.py:29
  125.6 5.8 copy-start
  125.6 144.5 %all-to-all-start = ((bf16[32,256,768]{2,0,1:T(8,128)(2,1)}), bf16[32,256,768]{2,0,1:T(8,128)(2,1)}, u32[]{:S(2)}, u32[]{:S(2)}) async-start(bf16[32,256,768]{2,0,1:T(8,128)(2,1)} %copy.15), calls=%async_computation | async-start | bytes 25165824 | tf_op jit(solution)/shard_map/all_to_all | solution.py:28
  131.1 1393.6 %reduce-scatter.2.cloned.1.call-start = ((), (), s32[]{:S(2)}) async-start(), calls=%async_computation.5 | async-start | bytes 10485760 | tf_op jit(solution)/shard_map/reduce_scatter | solution.py:58
  131.6 0.5 copy-start.2
  1366.5 14.7 copy-start.3
  1366.5 15.3 copy-start.1
Sparse Core Ops, SparseCore 0:
  1381.3 143.3 reduce-scatter.1
where the time goes:
time: 1540 us
  blocking collectives  827 us (54%)
  waiting for transfers between devices  274 us (18%)
  local copies, waits for them, and re-layouts  200 us (13%)
  matrix products  155 us (10%)
  other arithmetic  54.8 us (4%)
    all_to_all x1, blocking collectives, on_device(): lax.all_to_all(lax.all_to_all(slotted, 'lat', split_axis=1, concat_axis=2...  548 us
    all_to_all x1, blocking collectives, on_device(): lax.all_to_all(slotted, 'lat', split_axis=1, concat_axis=2, tiled=True)  278 us
    reduce_scatter x1, waiting for transfers between devices, on_device(): lax.psum_scatter(partial_value, 'lev', scatter_dimension=1, tiled=True)  141 us
    all_to_all x1, waiting for transfers between devices, on_device(): lax.all_to_all(spectra, 'lat', split_axis=1, concat_axis=0, tiled=True)  133 us
    dot_general x1, matrix products, on_device(): jnp.einsum('belx,xmc->lmcbe', fields, dft_table, precision=lax.Precision....  84.9 us
    all_to_all x2, local copies, waits for them, and re-layouts, on_device(): lax.all_to_all(lax.all_to_all(slotted, 'lat', split_axis=1, concat_axis=2...  68.5 us
    dot_general x1, matrix products, on_device(): jnp.einsum('esaql,fsaqk->selfk', blocks, blocks, preferred_element_type=j...  50.3 us
    all_to_all x2, local copies, waits for them, and re-layouts, on_device(): lax.all_to_all(slotted, 'lat', split_axis=1, concat_axis=2, tiled=True)  31.9 us
  transfers between devices with their start and end apart: 3, of which 2 were waited for; matrix products, arithmetic and copies ran while one was open for 7% of the time, Pallas kernels for 0%

commit v1 on v0

--- a/solution.py
+++ b/solution.py
@@ -1,8 +1,12 @@
+import functools
 import math
 
 import jax
 import jax.numpy as jnp
+import numpy as np
 from jax import lax
+from jax.experimental import pallas as pl
+from jax.experimental.pallas import tpu as pltpu
 from jax.sharding import PartitionSpec as P
 
 
@@ -15,7 +19,7 @@
     return jnp.stack([jnp.cos(angle) * factor, -jnp.sin(angle) * factor], axis=2)
 
 
-def on_device(fields, legendre, owner_counts):
+def plain_on_device(fields, legendre, owner_counts):
     members, lev_rows, lat_rows, points = fields.shape
     modes = legendre.shape[1]
     lev_count = lax.axis_size("lev")
@@ -64,9 +68,262 @@
     return jnp.where((offset < live_count)[:, None, None], scaled, jnp.zeros_like(scaled))
 
 
+LANES = 128
+VMEM_LIMIT = 60 * 1024 * 1024
+
+
+def split_bf16(values):
+    high = values.astype(jnp.bfloat16)
+    return high, (values - high.astype(jnp.float32)).astype(jnp.bfloat16)
+
+
+def folded_tables(points, orders):
+    tables = []
+    for residues, length in (((1, 3), points // 2), ((0,), points // 4), ((2,), points // 4)):
+        m = orders[np.isin(orders % 4, residues)]
+        angle = 2.0 * np.pi * ((m[:, None] * np.arange(length)[None, :]) % points) / points
+        table = np.concatenate([np.cos(angle), -np.sin(angle)]) * points ** -0.5
+        table = table.astype(np.float32)
+        high = table.astype(jnp.bfloat16)
+        low = (table - high.astype(np.float32)).astype(jnp.bfloat16)
+        tables.append(np.stack([high, low]))
+    return tables
+
+
+NT = (((1,), (1,)), ((), ()))
+TN = (((0,), (0,)), ((), ()))
+
+
+def dft_kernel(runs, width, pieces, *refs):
+    field_refs = refs[:pieces]
+    odd_ref, zero_ref, two_ref, out_ref, held = refs[pieces:]
+    rows, lats, _ = field_refs[0].shape
+    quarter = pieces * LANES // 4
+    lines = [ref.reshape(rows * lats, LANES) for ref in field_refs]
+
+    def fetch(lat):
+        return [
+            jnp.concatenate([line[pl.ds(lat + s, rows, lats), :] for s in range(2)], axis=0)
+            for line in lines
+        ]
+
+    def transform(table_ref, values):
+        high, low = split_bf16(values)
+        dot = functools.partial(lax.dot_general, dimension_numbers=NT, preferred_element_type=jnp.float32)
+        return dot(table_ref[0], high) + (dot(table_ref[1], high) + dot(table_ref[0], low))
+
+    def put(lat, lane, kind, sums):
+        count = sums.shape[0] // 2
+        for q in range(2):
+            done = 0
+            for start in runs[kind]:
+                held[q, pl.ds(start * lats + lat, width, lats), :] = (
+                    sums[q * count + done:q * count + done + width, lane:lane + LANES]
+                )
+                done += width
+
+    def step(pair, carry):
+        lat = 2 * pair
+        values = fetch(lat)
+        middle = len(values) // 2
+        even = jnp.concatenate([u + v for u, v in zip(values[:middle], values[middle:])], axis=1)
+        odd = jnp.concatenate([u - v for u, v in zip(values[:middle], values[middle:])], axis=1)
+        parts = (
+            transform(odd_ref, odd),
+            transform(zero_ref, even[:, :quarter] + even[:, quarter:]),
+            transform(two_ref, even[:, :quarter] - even[:, quarter:]),
+        )
+        for s in range(2):
+            for kind, sums in enumerate(parts):
+                put(lat + s, s * LANES, kind, sums)
+        return carry
+
+    lax.fori_loop(0, lats // 2, step, 0)
+    modes = out_ref.shape[0]
+    piece = 32
+
+    def emit(index, carry):
+        base = pl.multiple_of(index * piece, piece)
+        for q in range(2):
+            block = held[q, pl.ds(pl.multiple_of(base * lats, piece * lats), piece * lats), :]
+            block = block.astype(jnp.bfloat16).reshape(piece, lats, LANES)
+            out_ref[pl.ds(base, piece), :, q * LANES:(q + 1) * LANES] = block
+        return carry
+
+    lax.fori_loop(0, modes // piece, emit, 0)
+
+
+def dft(fields, lat_count, orders, modes):
+    members, lev_rows, lat_rows, points = fields.shape
+    rows = members * lev_rows
+    lats = 16
+    width = modes // lat_count
+    kinds = [[i for i in range(lat_count) if i % 4 in r] for r in ((1, 3), (0,), (2,))]
+    runs = [[i * width for i in kind] for kind in kinds]
+    tables = [jnp.asarray(t) for t in folded_tables(points, orders)]
+    groups = rows // LANES
+    pieces = points // LANES
+    return pl.pallas_call(
+        functools.partial(dft_kernel, runs, width, pieces),
+        grid=(lat_rows // lats, groups),
+        out_shape=jax.ShapeDtypeStruct((modes, lat_rows, 2 * rows), jnp.bfloat16),
+        in_specs=[
+            pl.BlockSpec((LANES, lats, LANES), functools.partial(lambda c, l, g: (g, l, c), c))
+            for c in range(pieces)
+        ]
+        + [pl.BlockSpec(t.shape, lambda l, g: (0, 0, 0)) for t in tables],
+        out_specs=pl.BlockSpec((modes, lats, 2 * LANES), lambda l, g: (0, l, g)),
+        scratch_shapes=[pltpu.VMEM((2, modes * lats, LANES), jnp.float32)],
+        compiler_params=pltpu.CompilerParams(vmem_limit_bytes=VMEM_LIMIT),
+        cost_estimate=pl.CostEstimate(flops=15_000_000_000, bytes_accessed=65_000_000, transcendentals=0),
+    )(*[fields.reshape(rows, lat_rows, points)] * pieces, *tables)
+
+
+def legendre_kernel(members, lev_rows, band, x_ref, l_ref, out_ref):
+    sources, _, slots, lat_rows, lanes = x_ref.shape
+    total = l_ref.shape[-1]
+    groups = lanes // (2 * LANES)
+    for a in range(slots):
+        x = x_ref[:, 0, a].reshape(sources * lat_rows, lanes)
+        table = l_ref[:, 0, a, :, band * a:]
+        table = table.reshape(sources * lat_rows, total - band * a)
+        waves = lax.dot_general(table, x, TN, preferred_element_type=jnp.float32)
+        for t in range(a, slots):
+            block = waves[(t - a) * band:(t - a + 1) * band]
+            row = band * (t * (t + 1) // 2 + a)
+            for q in range(2):
+                parts = [block[:, (2 * g + q) * LANES:(2 * g + q + 1) * LANES] for g in range(groups)]
+                total_sum = functools.reduce(jnp.add, parts)
+                shift = LANES // 2
+                while shift >= lev_rows:
+                    total_sum = total_sum + pltpu.roll(total_sum, shift, 1)
+                    shift //= 2
+                mean = total_sum * (1.0 / members)
+                for g in range(groups):
+                    out_ref[0, row:row + band, (2 * g + q) * LANES:(2 * g + q + 1) * LANES] = (
+                        parts[g] - mean
+                    ).astype(jnp.bfloat16)
+
+
+def covariance_kernel(band, slots, lev_rows, x_ref, out_ref, held):
+    sources, _, lanes = x_ref.shape
+    pack = LANES // lev_rows
+    groups = lanes // LANES
+    per_slot = groups * pack
+    for t in range(slots):
+        start = band * (t * (t + 1) // 2)
+
+        def spread(a, carry):
+            row = pl.multiple_of(start + a * band, band)
+            for g in range(groups):
+                parts = [
+                    x_ref[v, pl.ds(row, band), g * LANES:(g + 1) * LANES].astype(jnp.float32)
+                    for v in range(sources)
+                ]
+                for s in range(pack):
+                    joined = jnp.concatenate(
+                        [p[:, s * lev_rows:(s + 1) * lev_rows] for p in parts], axis=1
+                    )
+                    place = (a * per_slot + g * pack + s) * band
+                    held[pl.ds(pl.multiple_of(place, band), band), :] = joined
+            return carry
+
+        lax.fori_loop(0, t + 1, spread, 0)
+        depth = (t + 1) * per_slot
+
+        def multiply(n, carry):
+            for s in range(4):
+                each = n * 4 + s
+                values = held[pl.ds(each, depth, band), :].astype(jnp.bfloat16)
+                product = lax.dot_general(values, values, TN, preferred_element_type=jnp.float32)
+                out_ref[t * band + each] = product.astype(jnp.bfloat16)
+            return carry
+
+        lax.fori_loop(0, band // 4, multiply, 0)
+
+
+def exchange(values, axis):
+    return lax.all_to_all(values, axis, split_axis=0, concat_axis=0, tiled=True)
+
+
+def on_device(lat_count, lev_count, fields, legendre, owner_counts):
+    members, lev_rows, lat_rows, points = fields.shape
+    modes, totals = legendre.shape[1:]
+    owners = owner_counts.shape[0]
+    capacity = 2 * modes // owners
+    levels = lev_count * lev_rows
+    band = lat_count * lev_count
+    slots = modes // band
+    lanes = 2 * members * lev_rows
+    orders = np.arange(modes).reshape(slots, lev_count, lat_count).transpose(2, 1, 0).reshape(-1)
+
+    table = legendre.reshape(lat_rows, slots, lev_count, lat_count, totals).transpose(3, 2, 1, 0, 4)
+    table = exchange(table, "lat")
+    spectra = dft(fields, lat_count, orders, modes)
+    spectra = exchange(spectra.reshape(lat_count, lev_count, slots, lat_rows, lanes), "lat")
+
+    rows = band * slots * (slots + 1) // 2
+    anomaly = pl.pallas_call(
+        functools.partial(legendre_kernel, members, lev_rows, band),
+        grid=(lev_count,),
+        out_shape=jax.ShapeDtypeStruct((lev_count, rows, lanes), jnp.bfloat16),
+        in_specs=[
+            pl.BlockSpec((lat_count, 1, slots, lat_rows, lanes), lambda j: (0, j, 0, 0, 0)),
+            pl.BlockSpec((lat_count, 1, slots, lat_rows, totals), lambda j: (0, j, 0, 0, 0)),
+        ],
+        out_specs=pl.BlockSpec((1, rows, lanes), lambda j: (j, 0, 0)),
+        compiler_params=pltpu.CompilerParams(vmem_limit_bytes=VMEM_LIMIT),
+        cost_estimate=pl.CostEstimate(flops=4_000_000_000, bytes_accessed=24_000_000, transcendentals=0),
+    )(spectra, table)
+    anomaly = exchange(anomaly, "lev")
+
+    partial_value = pl.pallas_call(
+        functools.partial(covariance_kernel, band, slots, lev_rows),
+        out_shape=jax.ShapeDtypeStruct((totals, levels, levels), jnp.bfloat16),
+        in_specs=[pl.BlockSpec(memory_space=pltpu.VMEM)],
+        out_specs=pl.BlockSpec(memory_space=pltpu.VMEM),
+        scratch_shapes=[pltpu.VMEM((slots * 2 * members * band, levels), jnp.float32)],
+        compiler_params=pltpu.CompilerParams(vmem_limit_bytes=VMEM_LIMIT),
+        cost_estimate=pl.CostEstimate(flops=2_000_000_000, bytes_accessed=16_000_000, transcendentals=0),
+    )(anomaly)
+
+    share = totals // lat_count
+    partial_value = exchange(partial_value.reshape(lat_count, share, levels, levels), "lat")
+    summed = jnp.sum(partial_value.astype(jnp.float32), axis=0)
+    summed = summed.reshape(share, lev_count, lev_rows, levels).transpose(1, 0, 2, 3)
+    summed = exchange(summed.astype(jnp.bfloat16), "lev")
+    full = jnp.sum(summed.astype(jnp.float32), axis=0)
+    full = jnp.broadcast_to(full.astype(jnp.bfloat16)[None], (lat_count, share, lev_rows, levels))
+    full = exchange(full, "lat").reshape(totals, lev_rows, levels)
+
+    starts = jnp.cumsum(owner_counts) - owner_counts
+    owner = lax.axis_index("lat")
+    offset = jnp.arange(capacity, dtype=jnp.int32)
+    wavenumber = starts[owner] + offset
+    live = offset < owner_counts[owner]
+    chosen = jnp.take(full, jnp.where(live, wavenumber, 0), axis=0).astype(jnp.float32)
+    divisor = ((members - 1) * (2 * wavenumber + 2)).astype(jnp.float32)
+    return jnp.where(live[:, None, None], chosen / divisor[:, None, None], jnp.zeros_like(chosen))
+
+
+def pick(lat_count, lev_count, fields, legendre, owner_counts):
+    members, lev_rows, lat_rows, points = fields.shape
+    modes = legendre.shape[1]
+    fits = (
+        lat_rows % 16 == 0
+        and members * lev_rows % LANES == 0
+        and lev_rows * lev_count == LANES
+        and lat_count % 4 == 0
+        and modes % (lat_count * lev_count) == 0
+    )
+    if fits:
+        return on_device(lat_count, lev_count, fields, legendre, owner_counts)
+    return plain_on_device(fields, legendre, owner_counts)
+
+
 def solution(mesh):
     return jax.shard_map(
-        on_device,
+        functools.partial(pick, mesh.shape["lat"], mesh.shape["lev"]),
         mesh=mesh,
         in_specs=(P(None, "lev", "lat", None), P("lat", None, None), P()),
         out_specs=P("lat", "lev", None),

time: 1540 us -> 604 us (0.39)
  blocking collectives: 827 us -> 436 us
  waiting for transfers between devices: 274 us -> 21.9 us
  local copies, waits for them, and re-layouts: 200 us -> 10.1 us
  matrix products: 155 us -> 0 us
  Pallas kernels: 0 us -> 116 us
  other arithmetic: 54.8 us -> 10.1 us
    all_to_all x2 -> x4, blocking collectives: 827 us -> 436 us  [exchange(): return lax.all_to_all(values, axis, split_axis=0, concat_axis=0, tiled=True)]
    dot_general x3 -> x0, matrix products: 155 us -> none  [the longest x1 84.9 us: on_device(): jnp.einsum('belx,xmc->lmcbe', fields, dft_table, precision=lax.Precision....]
    reduce_scatter x1 -> x0, waiting for transfers between devices: 141 us -> none  [on_device(): lax.psum_scatter(partial_value, 'lev', scatter_dimension=1, tiled=True)]
    all_to_all x6 -> x0, local copies, waits for them, and re-layouts: 119 us -> none  [the longest x2 68.5 us: on_device(): lax.all_to_all(lax.all_to_all(slotted, 'lat', split_axis=1, concat_axis=2...]
    pallas_call x0 -> x3, Pallas kernels: none -> 116 us  [the longest x1 64 us: dft(): pl.pallas_call(functools.partial(dft_kernel, runs, width, pieces), grid=(...]
    all_to_all x2, waiting for transfers between devices: 133 us -> 21.9 us  [exchange(): return lax.all_to_all(values, axis, split_axis=0, concat_axis=0, tiled=True)]
    convert_element_type x2 -> x1, local copies, waits for them, and re-layouts: 35 us -> 0.09 us  [on_device(): summed = exchange(summed.astype(jnp.bfloat16), 'lev')]
    select_n x3 -> x2, other arithmetic: 23.9 us -> 2.51 us  [the longest x1 1.27 us: on_device(): jnp.take(full, jnp.where(live, wavenumber, 0), axis=0).astype(jnp.float32)]
  transfers between devices with their start and end apart: 3 -> 2, of which waited for: 2 -> 1; matrix products, arithmetic and copies ran while one was open for 7% -> 1% of each run, Pallas kernels for 0% -> 11%
where the time goes in v1:
time: 604 us; the launch traced here: 603 us
  blocking collectives  436 us (72%)
  Pallas kernels  116 us (19%)
  waiting for transfers between devices  21.9 us (4%)
  local copies, waits for them, and re-layouts  10.1 us (2%)
  other arithmetic  10.1 us (2%)
  starting transfers between devices  8.8 us (1%)
    all_to_all x4, blocking collectives, exchange(): return lax.all_to_all(values, axis, split_axis=0, concat_axis=0, tiled=True)  436 us
    pallas_call x1, Pallas kernels, dft(): pl.pallas_call(functools.partial(dft_kernel, runs, width, pieces), grid=(...  64 us
    pallas_call x1, Pallas kernels, on_device(): pl.pallas_call(functools.partial(covariance_kernel, band, slots, lev_rows...  34.9 us
    all_to_all x2, waiting for transfers between devices, exchange(): return lax.all_to_all(values, axis, split_axis=0, concat_axis=0, tiled=True)  21.9 us
    pallas_call x1, Pallas kernels, on_device(): pl.pallas_call(functools.partial(legendre_kernel, members, lev_rows, band...  17.5 us
  transfers between devices with their start and end apart: 2, of which 1 were waited for; matrix products, arithmetic and copies ran while one was open for 1% of the time, Pallas kernels for 11%

profile of v1, /device:TPU:0, one launch (start us, length us, event | category | flops | bytes accessed | tf_op | source)
XLA Modules:
  0.0 603.3 jit_solution(16903719175058027787)
XLA Ops:
  0.0 6.5 %copy.12 = bf16[32,8,4,8,256]{4,0,1,2,3:T(8,128)(2,1)} copy(bf16[32,8,4,8,256]{4,3,2,1,0:T(8,128)(2,1)} %bitcast.30) | data formatting | bytes 8388608 | tf_op jit(solution)/shard_map/reshape | solution.py:260
  6.5 5.2 all-to-all-start.1
  11.7 64.0 %shard_map.64 = bf16[256,32,768]{2,1,0:T(8,128)(2,1)} custom-call(f32[384,32,1024]{2,1,0:T(8,128)} %bitcast.18, f32[384,32,1024]{2,1,0:T(8,128)} %bitcast.19, f32[384,32,1024]{2,1,0:T(8,128)} %bitcast.20, f32[384,32,1024]{2,1,0:T(8,128)} %bitcast.21, f32[384,32,1024]{2,1,0:T(8,128)} %bitcast.22, f32[384,32,1024]{2,1,0:T(8,128)} %bitcast.23, ...), custom_call_target="tpu_custom_call" | custom-call | flops 15000000512 | bytes 65000000 | tf_op jit(solution)/shard_map/pallas_call | solution.py:166
  75.7 0.0 all-to-all-done.1.l_ref
  75.7 145.8 %all_to_all.30.x_ref = bf16[8,4,8,32,768]{4,3,2,1,0:T(8,128)(2,1)} all-to-all(bf16[8,4,8,32,768]{4,3,2,1,0:T(8,128)(2,1)} %bitcast.26), channel_id=1, replica_groups=mesh['lat'=8,'lev'=4] {'lat'}, dimensions={0} | all-to-all | bytes 25165824 | tf_op jit(solution)/shard_map/all_to_all | solution.py:246
  221.4 17.5 %shard_map.65 = bf16[4,1152,768]{2,1,0:T(8,128)(2,1)} custom-call(bf16[8,4,8,32,768]{4,3,2,1,0:T(8,128)(2,1)} %all_to_all.30.x_ref, bf16[8,4,8,32,256]{4,3,2,1,0:T(8,128)(2,1)} %all-to-all-done.1.l_ref), custom_call_target="tpu_custom_call" | custom-call | flops 4000000000 | bytes 24000000 | tf_op jit(solution)/shard_map/pallas_call | solution.py:266
  239.0 162.5 %all_to_all.31.x_ref = bf16[4,1152,768]{2,1,0:T(8,128)(2,1)} all-to-all(bf16[4,1152,768]{2,1,0:T(8,128)(2,1)} %shard_map.65), channel_id=1, replica_groups=mesh['lat'=8,'lev'=4] {'lev'}, dimensions={0} | all-to-all | bytes 14155776 | tf_op jit(solution)/shard_map/all_to_all | solution.py:246
  401.5 34.9 %shard_map.66 = bf16[256,128,128]{2,1,0:T(8,128)(2,1)} custom-call(bf16[4,1152,768]{2,1,0:T(8,128)(2,1)} %all_to_all.31.x_ref), custom_call_target="tpu_custom_call" | custom-call | flops 2000000000 | bytes 16000000 | tf_op jit(solution)/shard_map/pallas_call | solution.py:280
  436.3 99.7 %all_to_all.32 = bf16[8,32,128,128]{3,2,1,0:T(8,128)(2,1)} all-to-all(bf16[8,32,128,128]{3,2,1,0:T(8,128)(2,1)} %bitcast.27), channel_id=1, replica_groups=mesh['lat'=8,'lev'=4] {'lat'}, dimensions={0} | all-to-all | bytes 16777216 | tf_op jit(solution)/shard_map/all_to_all | solution.py:246
  536.1 5.2 reduce_sum.24
  541.3 0.0 copy-start
  541.3 0.1 copy.10
  541.4 27.9 %all_to_all.33 = bf16[4,32,32,128]{3,2,1,0:T(8,128)(2,1)S(1)} all-to-all(bf16[4,32,32,128]{3,2,1,0:T(8,128)(2,1)S(1)} %copy.10), channel_id=1, replica_groups=mesh['lat'=8,'lev'=4] {'lev'}, dimensions={0} | all-to-all | bytes 2097152 | tf_op jit(solution)/shard_map/all_to_all | solution.py:246
  569.3 0.2 reduce_sum.25
  569.5 1.7 broadcast_in_dim.38
  571.2 3.6 all-to-all-start.5
  574.8 0.0 copy-done
  574.8 0.2 reduce-window.9
  575.0 0.6 dynamic_slice.6
  575.6 0.6 dynamic_slice.7
  576.2 0.7 multiply_convert_fusion
  576.9 1.3 fusion
  578.1 1.3 compare_and_fusion
  579.4 21.9 %all-to-all-done.5 = bf16[8,32,32,128]{3,2,1,0:T(8,128)(2,1)S(1)} async-done(((bf16[8,32,32,128]{3,2,1,0:T(8,128)(2,1)}), bf16[8,32,32,128]{3,2,1,0:T(8,128)(2,1)S(1)}, u32[]{:S(2)}, u32[]{:S(2)}) %all-to-all-start.5) | async-done | bytes 2097184 | tf_op jit(solution)/shard_map/all_to_all | solution.py:246
  601.4 0.7 gather_fusion
  602.0 1.2 divide_select_fusion
  (2 shorter events, 0.0 us)
Async XLA Ops:
  6.5 69.2 %all-to-all-start.1 = ((bf16[8,4,8,32,256]{4,3,2,1,0:T(8,128)(2,1)}), bf16[8,4,8,32,256]{4,3,2,1,0:T(8,128)(2,1)}, u32[]{:S(2)}, u32[]{:S(2)}) async-start(bf16[8,4,8,32,256]{4,3,2,1,0:T(8,128)(2,1)} %bitcast.28), calls=%async_computation.1 | async-start | bytes 8388608 | tf_op jit(solution)/shard_map/all_to_all | solution.py:246
  541.3 33.5 %copy-start = (s32[8]{0:T(128)S(1)}, s32[8]{0:T(128)}, u32[]{:S(2)}) copy-start(s32[8]{0:T(128)} %param.8) | copy-start | bytes 100
  571.2 30.2 %all-to-all-start.5 = ((bf16[8,32,32,128]{3,2,1,0:T(8,128)(2,1)}), bf16[8,32,32,128]{3,2,1,0:T(8,128)(2,1)S(1)}, u32[]{:S(2)}, u32[]{:S(2)}) async-start(bf16[8,32,32,128]{3,2,1,0:T(8,128)(2,1)} %broadcast_in_dim.38), calls=%async_computation.5 | async-start | bytes 4194304 | tf_op jit(solution)/shard_map/all_to_all | solution.py:246
